TPU v7x, 32 devices: a 4x4x1 block of a 4x4x8 slice. The times are simulated.
32 devices in a mesh: rep: 2 (over z, core), dp: 16 (over x, y).
Axes of the slice: x: 4, y: 4, z: 1, core: 2. Of those that a mesh axis runs over, the one named last changes fastest.
The devices are a block of a 4x4x8 slice.
Arguments:
- g_w_gate: bfloat16 [32, 2, 1024, 4096], P(('rep', 'dp')), parts along dimension 0
- g_w_up: bfloat16 [32, 2, 1024, 4096], P(('rep', 'dp')), parts along dimension 0
- g_w_down: bfloat16 [32, 2, 4096, 1024], P(('rep', 'dp')), parts along dimension 0
- w_gate: bfloat16 [2, 1024, 4096], replicated
- w_up: bfloat16 [2, 1024, 4096], replicated
- w_down: bfloat16 [2, 4096, 1024], replicated
- m_w_gate: float32 [2, 1024, 4096], P(None, 'dp')
- m_w_up: float32 [2, 1024, 4096], P(None, 'dp')
- m_w_down: float32 [2, 4096, 1024], P(None, 'dp')
- v_w_gate: float32 [2, 1024, 4096], P(None, 'dp')
- v_w_up: float32 [2, 1024, 4096], P(None, 'dp')
- v_w_down: float32 [2, 4096, 1024], P(None, 'dp')
Outputs:
- output 1: bfloat16 [4, 1024, 4096], P('rep'), parts along dimension 0
- output 2: bfloat16 [4, 1024, 4096], P('rep'), parts along dimension 0
- output 3: bfloat16 [4, 4096, 1024], P('rep'), parts along dimension 0
- output 4: float32 [4, 1024, 4096], P('rep', 'dp'), parts along dimension 0
- output 5: float32 [4, 1024, 4096], P('rep', 'dp'), parts along dimension 0
- output 6: float32 [4, 4096, 1024], P('rep', 'dp'), parts along dimension 0
- output 7: float32 [4, 1024, 4096], P('rep', 'dp'), parts along dimension 0
- output 8: float32 [4, 1024, 4096], P('rep', 'dp'), parts along dimension 0
- output 9: float32 [4, 4096, 1024], P('rep', 'dp'), parts along dimension 0
There are 2 independent parts. A program takes and returns all parts, laid end to end along the dimension named above; an argument that names none is the same for every part.
All inputs are finite; a program needn't handle non-finite values.
Results may differ from a plain program's by a relative error of at most 0.022.
Values are sent between devices in bfloat16 or wider.
A program may use at most 768 MiB of HBM per device.

v0:
```python
import jax
import jax.numpy as jnp
from jax import lax
from jax.sharding import PartitionSpec as P


def adamw(w, m, v, g):
    m = 0.9 * m + 0.1 * g
    v = 0.95 * v + 0.05 * g * g
    step = m * lax.rsqrt(v + 1e-8) + 0.1 * w
    return (w - 0.02 * step).astype(jnp.bfloat16), m, v


def solution(mesh):
    def step(*arrays):
        terms, weights, m, v = (arrays[i : i + 3] for i in (0, 3, 6, 9))
        gradients = [lax.psum_scatter(t[0], "dp", scatter_dimension=1, tiled=True).astype(jnp.float32) for t in terms]
        me = lax.axis_index("dp")
        own = [lax.dynamic_slice_in_dim(w, me * one.shape[1], one.shape[1], 1).astype(jnp.float32) for w, one in zip(weights, m, strict=True)]
        new = [adamw(w, m, v, g) for w, m, v, g in zip(own, m, v, gradients, strict=True)]
        whole = [lax.all_gather(one[0], "dp", axis=1, tiled=True) for one in new]
        return (*whole, *(one[1] for one in new), *(one[2] for one in new))

    all_of, cut = P(None, None, None), P(None, "dp", None)
    return jax.shard_map(
        step,
        mesh=mesh,
        in_specs=(P(("rep", "dp"), None, None, None),) * 3 + (all_of,) * 3 + (cut,) * 6,
        out_specs=(P("rep", None, None),) * 3 + (P("rep", "dp", None),) * 6,
        check_vma=False,
    )
```

profile of v0, /device:TPU:97, one launch (start us, length us, event | category | flops | bytes accessed | tf_op | source)
XLA Modules:
  0.0 700.9 jit_solution(15981728538426444772)
XLA Ops:
  7.2 0.1 reduce-scatter.8.cloned.1.call-start
  7.3 0.7 reduce-scatter.8.cloned.1.call-update
  8.0 0.1 reduce-scatter.6.cloned.1.call-start
  8.1 0.7 reduce-scatter.6.cloned.1.call-update
  8.8 0.1 reduce-scatter.4.cloned.1.call-start
  8.9 0.0 copy-start.1
  8.9 0.7 reduce-scatter.4.cloned.1.call-update
  9.6 0.1 all-gather.8.cloned.1.call-start
  9.7 110.2 %reduce-scatter.8.cloned.1.call-done = bf16[2,256,1024]{2,1,0:T(8,128)(2,1)} async-done(((bf16[2,4096,1024]{2,1,0:T(8,128)(2,1)}), bf16[2,256,1024]{2,1,0:T(8,128)(2,1)}) %reduce-scatter.8.cloned.1.call-update) | async-done | bytes 1048592 | tf_op jit(solution)/shard_map/reduce_scatter | solution.py:17
  119.9 0.0 copy-done.1
  119.9 5.3 fusion.10
  125.2 0.1 all-gather.8.cloned.1.call-update
  125.2 0.1 all-gather.6.cloned.1.call-start
  125.3 102.8 %reduce-scatter.6.cloned.1.call-done = bf16[2,64,4096]{2,1,0:T(8,128)(2,1)} async-done(((bf16[2,1024,4096]{2,1,0:T(8,128)(2,1)}), bf16[2,64,4096]{2,1,0:T(8,128)(2,1)}) %reduce-scatter.6.cloned.1.call-update) | async-done | bytes 1048592 | tf_op jit(solution)/shard_map/reduce_scatter | solution.py:17
  228.1 0.0 copy-start.2
  228.1 5.9 fusion.6
  234.0 0.1 all-gather.6.cloned.1.call-update
  234.1 0.1 all-gather.4.cloned.1.call-start
  234.1 102.1 %reduce-scatter.4.cloned.1.call-done = bf16[2,64,4096]{2,1,0:T(8,128)(2,1)} async-done(((bf16[2,1024,4096]{2,1,0:T(8,128)(2,1)}), bf16[2,64,4096]{2,1,0:T(8,128)(2,1)}) %reduce-scatter.4.cloned.1.call-update) | async-done | bytes 1048592 | tf_op jit(solution)/shard_map/reduce_scatter | solution.py:17
  336.2 0.0 copy-done.2
  336.2 5.2 fusion.2
  341.4 0.1 all-gather.4.cloned.1.call-update
  341.4 102.9 %all-gather.8.cloned.1.call-done = bf16[2,4096,1024]{2,1,0:T(8,128)(2,1)} async-done(((bf16[2,256,1024]{2,1,0:T(8,128)(2,1)}), bf16[2,4096,1024]{2,1,0:T(8,128)(2,1)}) %all-gather.8.cloned.1.call-update) | async-done | bytes 16777232 | tf_op jit(solution)/shard_map/all_gather | solution.py:21
  444.3 107.8 %all-gather.6.cloned.1.call-done = bf16[2,1024,4096]{2,1,0:T(8,128)(2,1)} async-done(((bf16[2,64,4096]{2,1,0:T(8,128)(2,1)}), bf16[2,1024,4096]{2,1,0:T(8,128)(2,1)}) %all-gather.6.cloned.1.call-update) | async-done | bytes 16777232 | tf_op jit(solution)/shard_map/all_gather | solution.py:21
  552.1 107.8 %all-gather.4.cloned.1.call-done = bf16[2,1024,4096]{2,1,0:T(8,128)(2,1)} async-done(((bf16[2,64,4096]{2,1,0:T(8,128)(2,1)}), bf16[2,1024,4096]{2,1,0:T(8,128)(2,1)}) %all-gather.4.cloned.1.call-update) | async-done | bytes 16777232 | tf_op jit(solution)/shard_map/all_gather | solution.py:21
  659.9 0.0 copy-start
  659.9 0.0 slice-start
  659.9 0.0 slice-start.1
  659.9 0.0 slice-start.2
  659.9 16.8 %copy.24 = bf16[2,1024,4096]{2,1,0:T(8,128)(2,1)} copy(bf16[2,1024,4096]{2,1,0:T(8,128)(2,1)} %all-gather.4.cloned.1.call-done) | data formatting | bytes 33554432
  676.7 0.0 copy-done
  676.7 0.0 slice-start.3
  676.7 8.5 %copy.25 = bf16[2,1024,4096]{2,1,0:T(8,128)(2,1)} copy(bf16[2,1024,4096]{2,1,0:T(8,128)(2,1)S(1)} %copy-done) | data formatting | bytes 33554432
  685.2 0.0 slice-done
  685.2 0.0 slice-done.1
  685.2 1.2 slice-done.2
  686.4 1.4 slice-done.3
  687.8 6.2 copy.26
  (1 shorter events, 0.0 us)
Async XLA Ops:
  7.2 112.7 %reduce-scatter.8.cloned.1.call-start = ((), (), s32[]{:S(2)}) async-start(), calls=%async_computation.7 | async-start | bytes 17825792 | tf_op jit(solution)/shard_map/reduce_scatter | solution.py:17
  8.0 220.1 %reduce-scatter.6.cloned.1.call-start = ((), (), s32[]{:S(2)}) async-start(), calls=%async_computation.5 | async-start | bytes 17825792 | tf_op jit(solution)/shard_map/reduce_scatter | solution.py:17
  8.8 327.4 %reduce-scatter.4.cloned.1.call-start = ((), (), s32[]{:S(2)}) async-start(), calls=%async_computation.3 | async-start | bytes 17825792 | tf_op jit(solution)/shard_map/reduce_scatter | solution.py:17
  8.9 111.0 %copy-start.1 = (f32[2,256,1024]{2,1,0:T(8,128)S(1)}, f32[2,256,1024]{2,1,0:T(8,128)}, u32[]{:S(2)}) copy-start(f32[2,256,1024]{2,1,0:T(8,128)} %param.23) | copy-start | bytes 6291460
  9.6 434.7 %all-gather.8.cloned.1.call-start = ((), (), s32[]{:S(2)}) async-start(), calls=%async_computation.8 | async-start | bytes 17825792 | tf_op jit(solution)/shard_map/all_gather | solution.py:21
  125.2 426.9 %all-gather.6.cloned.1.call-start = ((), (), s32[]{:S(2)}) async-start(), calls=%async_computation.6 | async-start | bytes 17825792 | tf_op jit(solution)/shard_map/all_gather | solution.py:21
  228.1 108.2 %copy-start.2 = (f32[2,64,4096]{2,1,0:T(8,128)S(1)}, f32[2,64,4096]{2,1,0:T(8,128)}, u32[]{:S(2)}) copy-start(f32[2,64,4096]{2,1,0:T(8,128)} %param.21) | copy-start | bytes 6291460
  234.1 425.9 %all-gather.4.cloned.1.call-start = ((), (), s32[]{:S(2)}) async-start(), calls=%async_computation.4 | async-start | bytes 17825792 | tf_op jit(solution)/shard_map/all_gather | solution.py:21
  659.9 16.8 %copy-start = (bf16[2,1024,4096]{2,1,0:T(8,128)(2,1)S(1)}, bf16[2,1024,4096]{2,1,0:T(8,128)(2,1)}, u32[]{:S(2)}) copy-start(bf16[2,1024,4096]{2,1,0:T(8,128)(2,1)} %all-gather.6.cloned.1.call-done) | copy-start | bytes 50331652
  659.9 25.3 %slice-start = ((s8[16777216]{0:T(1024)(128)(4,1)}), s8[4194304]{0:T(1024)(128)(4,1)S(1)}, s32[]{:S(2)}) async-start(s8[16777216]{0:T(1024)(128)(4,1)} %bitcast.6), calls=%async_computation.9 | async-start | bytes 8388608
  659.9 25.3 %slice-start.1 = ((s8[16777216]{0:T(1024)(128)(4,1)}), s8[4194304]{0:T(1024)(128)(4,1)S(1)}, s32[]{:S(2)}) async-start(s8[16777216]{0:T(1024)(128)(4,1)} %bitcast.6), calls=%async_computation.10 | async-start | bytes 8388608
  659.9 26.5 %slice-start.2 = ((s8[16777216]{0:T(1024)(128)(4,1)}), s8[4194304]{0:T(1024)(128)(4,1)S(1)}, s32[]{:S(2)}) async-start(s8[16777216]{0:T(1024)(128)(4,1)} %bitcast.6), calls=%async_computation.11 | async-start | bytes 8388608
  676.7 11.1 %slice-start.3 = ((s8[16777216]{0:T(1024)(128)(4,1)}), s8[4194304]{0:T(1024)(128)(4,1)S(1)}, s32[]{:S(2)}) async-start(s8[16777216]{0:T(1024)(128)(4,1)} %bitcast.6), calls=%async_computation.12 | async-start | bytes 8388608
Sparse Core Ops, SparseCore 0:
  11.2 108.6 reduce-scatter.7
  123.1 104.8 reduce-scatter.5
  231.3 104.8 reduce-scatter.3
  338.7 105.5 all-gather.7
  446.8 105.3 all-gather.5
  554.6 105.3 all-gather.3
where the time goes:
time: 701 us
  waiting for transfers between devices  636 us (91%)
  local copies, waits for them, and re-layouts  34.1 us (5%)
  other arithmetic  16.3 us (2%)
  between operations  14.2 us (2%)
    all_gather x3, waiting for transfers between devices, step(): whole = [lax.all_gather(one[0], 'dp', axis=1, tiled=True) for one in new]  318 us
    reduce_scatter x3, waiting for transfers between devices, step(): lax.psum_scatter(t[0], 'dp', scatter_dimension=1, tiled=True)  315 us
    unnamed x17, local copies, waits for them, and re-layouts  34.1 us
    convert_element_type x3, other arithmetic, adamw(): return ((w - 0.02 * step).astype(jnp.bfloat16), m, v)  16.3 us
  transfers between devices with their start and end apart: 6, of which 6 were waited for; matrix products, arithmetic and copies ran while one was open for 2% of the time, Pallas kernels for 0%

commit v1 on v0

v1 whole, which is shorter than its diff:
```python
import functools
import math

import jax
import jax.numpy as jnp
from jax import lax
from jax.experimental import pallas as pl
from jax.experimental.pallas import tpu as pltpu
from jax.sharding import PartitionSpec as P

MESH = pl.DeviceIdType.MESH
F32, BF16 = jnp.float32, jnp.bfloat16
STAGES = 9


def adamw(w, m, v, g):
    m = 0.9 * m + 0.1 * g
    v = 0.95 * v + 0.05 * g * g
    step = m * lax.rsqrt(v + 1e-8) + 0.1 * w
    return (w - 0.02 * step).astype(BF16), m, v


def step_kernel(side, piece, per_weight, *refs):
    n_w = 3
    grads, weights, ms, vs = (refs[i * n_w : (i + 1) * n_w] for i in range(4))
    wholes, new_ms, new_vs = (refs[i * n_w : (i + 1) * n_w] for i in range(4, 7))
    (l1, l2, m1, m2, o1, o2, w_in, m_io, v_io, kept, kept_half, w_new,
     send_sem, r_sem, ag_sem, o1_sem, o2_sem, in_sem, out_sem, own_sem) = refs[7 * n_w :]
    rows, cols = piece
    half = cols // 2
    chunks = n_w * per_weight
    me = lax.axis_index("dp")
    x, y = me // side, me % side

    def at(px, py):
        return {"dp": px * side + py}

    xs = [(x + 1) % side, (x + side - 1) % side]
    ys = [(y + 1) % side, (y + side - 1) % side]
    along_x, along_y = [at(i, y) for i in xs], [at(x, i) for i in ys]

    barrier = pltpu.get_barrier_semaphore()
    for device in along_x + along_y:
        pl.semaphore_signal(barrier, inc=1, device_id=device, device_id_type=MESH)
    pl.semaphore_wait(barrier, 4)

    layers = [
        dict(l=0, p=x, q=y, ps=xs, qs=ys, first=along_x, second=along_y),
        dict(l=1, p=y, q=x, ps=ys, qs=xs, first=along_y, second=along_x),
    ]

    def region(ref, k, part=None):
        if ref.shape[-2] == rows:
            row, col = pl.ds(0, rows), k * cols
        else:
            row, col = pl.ds(pl.multiple_of(k * rows, rows), rows), 0
        if part is None:
            return row, pl.ds(pl.multiple_of(col, cols) if not isinstance(col, int) else col, cols)
        col = col + part * half
        return row, pl.ds(pl.multiple_of(col, half) if not isinstance(col, int) else col, half)

    def block(ref, L, p, q, k, part=None):
        row, col = region(ref, k, part)
        return ref.at[(L["l"], p, q, row, col) if L["l"] == 0 else (L["l"], q, p, row, col)]

    def mine(ref, L, k):
        return ref.at[(L["l"], *region(ref, k))]

    def part_of(ref, part):
        return ref.at[..., pl.ds(part * half, half)]

    def for_weight(c, fn):
        for i in range(n_w):
            pl.when(c // per_weight == i)(functools.partial(fn, i, c % per_weight))

    def send(src, dst, s_sem, d_sem, device):
        pltpu.make_async_remote_copy(src, dst, s_sem, d_sem, device_id=device, device_id_type=MESH).start()

    def wait(ref, sem):
        pltpu.make_async_copy(ref, ref, sem).wait()

    every = pl.ds(0, side)

    def stage1(L, c):
        l = L["l"]

        def go(i, k):
            far = (L["p"] + 2) % side
            for d in range(2):
                send(block(grads[i], L, far, every, k, 1 - d), l1.at[c, l, d], send_sem.at[c, l, 0], r_sem.at[c, l, 0], L["first"][d])
            for d in range(2):
                send(block(grads[i], L, L["ps"][d], every, k, d), part_of(l2.at[c, l, d], d), send_sem.at[c, l, 0], r_sem.at[c, l, 1], L["first"][d])
                pltpu.make_async_copy(block(grads[i], L, L["ps"][d], every, k, 1 - d), o1.at[c % 2, l, d], o1_sem.at[c % 2, l, d]).start()

        for_weight(c, go)

    def stage2(L, c):
        l = L["l"]
        for_weight(c, lambda i, k: pltpu.make_async_copy(block(grads[i], L, L["p"], every, k), o2.at[c % 2, l], o2_sem.at[c % 2, l]).start())
        wait(l1.at[c, l], r_sem.at[c, l, 0])
        for d in range(2):
            wait(o1.at[c % 2, l, d], o1_sem.at[c % 2, l, d])

            @pl.loop(0, side * (rows // 16))
            def _(j):
                b, r = j // (rows // 16), pl.ds(pl.multiple_of(j % (rows // 16) * 16, 16), 16)
                l1[c, l, d, b, r, :] = (l1[c, l, d, b, r, :].astype(F32) + o1[c % 2, l, d, b, r, :].astype(F32)).astype(BF16)

            send(l1.at[c, l, d], part_of(l2.at[c, l, d], 1 - d), send_sem.at[c, l, 0], r_sem.at[c, l, 1], L["first"][d])

    def stage3(L, c):
        l, q = L["l"], L["q"]
        wait(l2.at[c, l], r_sem.at[c, l, 1])
        wait(o2.at[c % 2, l], o2_sem.at[c % 2, l])
        low, high = pl.ds(0, half), pl.ds(half, half)

        def total(b, r, col):
            return l2[c, l, 0, b, r, col].astype(F32) + l2[c, l, 1, b, r, col].astype(F32) + o2[c % 2, l, b, r, col].astype(F32)

        far = (q + 2) % side

        @pl.loop(0, rows // 16)
        def _(j):
            r = pl.ds(pl.multiple_of(j * 16, 16), 16)
            for col in (low, high):
                kept[c % 3, l, r, col] = total(q, r, col)
                l2[c, l, 0, far, r, col] = total(far, r, col).astype(BF16)
            for d, (direct, later) in enumerate(((low, high), (high, low))):
                near = L["qs"][d]
                kept_half[c % 3, l, d, r, :] = total(near, r, later)
                l2[c, l, 0, near, r, direct] = total(near, r, direct).astype(BF16)

        for d in range(2):
            send(part_of(l2.at[c, l, 0, far], 1 - d), m1.at[c, l, d], send_sem.at[c, l, 1], r_sem.at[c, l, 2], L["second"][d])
        for d in range(2):
            send(part_of(l2.at[c, l, 0, L["qs"][d]], d), part_of(m2.at[c, l, d], d), send_sem.at[c, l, 1], r_sem.at[c, l, 3], L["second"][d])

    def stage4(L, c):
        l = L["l"]

        def load(i, k):
            for ref, buffer, s in (
                (block(weights[i], L, L["p"], L["q"], k), w_in, 0),
                (mine(ms[i], L, k), m_io, 1),
                (mine(vs[i], L, k), v_io, 2),
            ):
                pltpu.make_async_copy(ref, buffer.at[c % 2, l], in_sem.at[c % 2, l, s]).start()

        @pl.when(c >= 2)
        def _():
            wait(m_io.at[c % 2, l], out_sem.at[c % 2, l, 0])
            wait(v_io.at[c % 2, l], out_sem.at[c % 2, l, 1])

        for_weight(c, load)
        wait(m1.at[c, l], r_sem.at[c, l, 2])
        for d in range(2):

            @pl.loop(0, rows // 16)
            def _(j):
                r = pl.ds(pl.multiple_of(j * 16, 16), 16)
                m1[c, l, d, r, :] = (m1[c, l, d, r, :].astype(F32) + kept_half[c % 3, l, d, r, :]).astype(BF16)

            send(m1.at[c, l, d], part_of(m2.at[c, l, d], 1 - d), send_sem.at[c, l, 1], r_sem.at[c, l, 3], L["second"][d])

    def stage5(L, c):
        l = L["l"]
        wait(m2.at[c, l], r_sem.at[c, l, 3])
        for s, buffer in enumerate((w_in, m_io, v_io)):
            wait(buffer.at[c % 2, l], in_sem.at[c % 2, l, s])

        @pl.loop(0, rows // 16)
        def _(j):
            r = pl.ds(pl.multiple_of(j * 16, 16), 16)
            g = kept[c % 3, l, r, :] + m2[c, l, 0, r, :].astype(F32) + m2[c, l, 1, r, :].astype(F32)
            g = g.astype(BF16).astype(F32)
            w_new[c, l, r, :], m_io[c % 2, l, r, :], v_io[c % 2, l, r, :] = adamw(
                w_in[c % 2, l, r, :].astype(F32), m_io[c % 2, l, r, :], v_io[c % 2, l, r, :], g
            )

        def go(i, k):
            there = block(wholes[i], L, L["p"], L["q"], k)
            for d in range(2):
                send(w_new.at[c, l], there, send_sem.at[c, l, 2], ag_sem.at[c, l, d], L["second"][d])
            pltpu.make_async_copy(w_new.at[c, l], there, own_sem.at[c % 3, l]).start()
            pltpu.make_async_copy(m_io.at[c % 2, l], mine(new_ms[i], L, k), out_sem.at[c % 2, l, 0]).start()
            pltpu.make_async_copy(v_io.at[c % 2, l], mine(new_vs[i], L, k), out_sem.at[c % 2, l, 1]).start()

        for_weight(c, go)

    def stage6(L, c):
        l = L["l"]

        def go(i, k):
            for d in range(2):
                wait(w_new.at[c, l], ag_sem.at[c, l, d])
                there = block(wholes[i], L, L["p"], L["qs"][1 - d], k, 1 - d)
                send(there, there, send_sem.at[c, l, 2], ag_sem.at[c, l, 2 + d], L["second"][d])

        for_weight(c, go)

    def stage7(L, c):
        l = L["l"]
        wait(w_new.at[c, l], own_sem.at[c % 3, l])
        for d in range(2):
            wait(part_of(w_new.at[c, l], d), ag_sem.at[c, l, 2 + d])

        def go(i, k):
            there = block(wholes[i], L, L["p"], every, k)
            for d in range(2):
                send(there, there, send_sem.at[c, l, 3], ag_sem.at[c, l, 4 + d], L["first"][d])

        for_weight(c, go)

    def stage8(L, c):
        l = L["l"]

        def go(i, k):
            for d in range(2):
                wait(o2.at[0, 0], ag_sem.at[c, l, 4 + d])
                there = block(wholes[i], L, L["ps"][1 - d], every, k, 1 - d)
                send(there, there, send_sem.at[c, l, 3], ag_sem.at[c, l, 6 + d], L["first"][d])

        for_weight(c, go)

    def stage9(L, c):
        l = L["l"]
        for d in range(2):
            wait(o1.at[0, 0, 0], ag_sem.at[c, l, 6 + d])

    stages = (stage1, stage2, stage3, stage4, stage5, stage6, stage7, stage8, stage9)

    @pl.loop(0, chunks + STAGES - 1)
    def _(t):
        for s, stage in enumerate(stages):
            c = t - s

            @pl.when((c >= 0) & (c < chunks))
            def _():
                for L in layers:
                    stage(L, c)

    for L in layers:
        for c in (chunks - 2, chunks - 1):
            wait(m_io.at[c % 2, L["l"]], out_sem.at[c % 2, L["l"], 0])
            wait(v_io.at[c % 2, L["l"]], out_sem.at[c % 2, L["l"], 1])

    three, row, col = pl.ds(0, 3), pl.ds(0, rows), pl.ds(0, cols)

    @pl.loop(0, chunks)
    def _(c):
        for l in range(2):
            wait(wholes[0].at[l, three, every, row, col], send_sem.at[c, l, 0])
            wait(wholes[0].at[l, 0, three, row, col], send_sem.at[c, l, 1])
            wait(wholes[0].at[l, 0, three, row, col], send_sem.at[c, l, 2])
            wait(wholes[0].at[l, three, every, row, col], send_sem.at[c, l, 3])


def solution(mesh):
    n = mesh.shape["dp"]
    side = math.isqrt(n)

    def step(*arrays):
        terms, weights, m, v = (arrays[i : i + 3] for i in (0, 3, 6, 9))
        layers = m[0].shape[0]
        piece = tuple(min(one.shape[i] for one in m) for i in (1, 2))
        rows, cols = piece
        sizes = {one.shape[1] * one.shape[2] for one in m}
        assert side * side == n and side == 4 and layers == 2 and len(sizes) == 1
        per_weight = sizes.pop() // (rows * cols)
        chunks = 3 * per_weight

        def blocks(a, one):
            return a.reshape(layers, side, side, *one.shape[1:])

        inputs = [blocks(a, one) for a, one in zip(terms, m)] + [blocks(a, one) for a, one in zip(weights, m)] + [*m, *v]
        outs = [jax.ShapeDtypeStruct((layers, side, side, *one.shape[1:]), BF16) for one in m]
        outs += [jax.ShapeDtypeStruct(one.shape, F32) for one in (*m, *v)]
        half = cols // 2
        dma = pltpu.SemaphoreType.DMA
        any_space = pl.BlockSpec(memory_space=pl.ANY)
        results = pl.pallas_call(
            functools.partial(step_kernel, side, piece, per_weight),
            out_shape=outs,
            in_specs=[any_space] * 12,
            out_specs=[any_space] * 9,
            scratch_shapes=[
                pltpu.VMEM((chunks, layers, 2, side, rows, half), BF16),
                pltpu.VMEM((chunks, layers, 2, side, rows, cols), BF16),
                pltpu.VMEM((chunks, layers, 2, rows, half), BF16),
                pltpu.VMEM((chunks, layers, 2, rows, cols), BF16),
                pltpu.VMEM((2, layers, 2, side, rows, half), BF16),
                pltpu.VMEM((2, layers, side, rows, cols), BF16),
                pltpu.VMEM((2, layers, rows, cols), BF16),
                pltpu.VMEM((2, layers, rows, cols), F32),
                pltpu.VMEM((2, layers, rows, cols), F32),
                pltpu.VMEM((3, layers, rows, cols), F32),
                pltpu.VMEM((3, layers, 2, rows, half), F32),
                pltpu.VMEM((chunks, layers, rows, cols), BF16),
                dma((chunks, layers, 4)),
                dma((chunks, layers, 4)),
                dma((chunks, layers, 8)),
                dma((2, layers, 2)),
                dma((2, layers)),
                dma((2, layers, 3)),
                dma((2, layers, 2)),
                dma((3, layers)),
            ],
            compiler_params=pltpu.CompilerParams(collective_id=0, has_side_effects=True, vmem_limit_bytes=63 * 2**20),
            name="step",
        )(*inputs)
        whole = [r.reshape(a.shape) for r, a in zip(results[:3], weights)]
        return (*whole, *results[3:])

    all_of, cut = P(None, None, None), P(None, "dp", None)
    return jax.shard_map(
        step,
        mesh=mesh,
        in_specs=(P(("rep", "dp"), None, None, None),) * 3 + (all_of,) * 3 + (cut,) * 6,
        out_specs=(P("rep", None, None),) * 3 + (P("rep", "dp", None),) * 6,
        check_vma=False,
    )
```

time: 701 us -> 566 us (0.81)
  waiting for transfers between devices: 636 us -> 0 us
  Pallas kernels: 0 us -> 518 us
  other arithmetic: 16.3 us -> 0.01 us
  between operations: 14.2 us -> 0.7 us
  local copies, waits for them, and re-layouts: 34.1 us -> 47.2 us
    pallas_call x0 -> x1, Pallas kernels: none -> 518 us  [step(): pl.pallas_call(functools.partial(step_kernel, side, piece, per_weight), o...]
    all_gather x3 -> x0, waiting for transfers between devices: 318 us -> none  [step(): whole = [lax.all_gather(one[0], 'dp', axis=1, tiled=True) for one in new]]
    reduce_scatter x3 -> x0, waiting for transfers between devices: 315 us -> none  [step(): lax.psum_scatter(t[0], 'dp', scatter_dimension=1, tiled=True)]
    convert_element_type x3 -> x0, other arithmetic: 16.3 us -> none  [adamw(): return ((w - 0.02 * step).astype(jnp.bfloat16), m, v)]
    unnamed x17 -> x31, local copies, waits for them, and re-layouts: 34.1 us -> 47.2 us
  transfers between devices with their start and end apart: 6 -> 0, of which waited for: 6 -> 0; matrix products, arithmetic and copies ran while one was open for 2% -> 0% of each run, Pallas kernels for 0% -> 0%
where the time goes in v1:
time: 566 us
  Pallas kernels  518 us (92%)
  local copies, waits for them, and re-layouts  47.2 us (8%)
    pallas_call x1, Pallas kernels, step(): pl.pallas_call(functools.partial(step_kernel, side, piece, per_weight), o...  518 us
    unnamed x31, local copies, waits for them, and re-layouts  47.2 us

profile of v1, /device:TPU:97, one launch (start us, length us, event | category | flops | bytes accessed | tf_op | source)
XLA Modules:
  0.0 566.0 jit_solution(5804817215352734176)
XLA Ops:
  0.6 518.0 %step.1 = (bf16[2,4,4,64,4096]{4,3,2,1,0:T(8,128)(2,1)}, bf16[2,4,4,64,4096]{4,3,2,1,0:T(8,128)(2,1)}, bf16[2,4,4,256,1024]{4,3,2,1,0:T(8,128)(2,1)}, f32[2,64,4...) custom-call(bf16[2,4,4,64,4096]{4,3,2,1,0:T(8,128)(2,1)} %bitcast.9,, ...), custom_call_target="tpu_custom_call" | custom-call | tf_op jit(solution)/shard_map/step/pallas_call | solution.py:281
  518.7 0.0 copy-start
  518.7 0.0 slice-start
  518.7 0.0 slice-start.1
  518.7 16.8 %copy.30 = bf16[2,1024,4096]{2,1,0:T(8,128)(2,1)} copy(bf16[2,1024,4096]{2,1,0:T(8,128)(2,1)} %bitcast.19) | data formatting | bytes 33554432
  535.5 0.0 copy-done
  535.5 0.0 slice-start.2
  535.5 0.0 slice-start.3
  535.5 8.5 %copy.31 = bf16[2,1024,4096]{2,1,0:T(8,128)(2,1)} copy(bf16[2,1024,4096]{2,1,0:T(8,128)(2,1)S(1)} %bitcast.18) | data formatting | bytes 33554432
  544.0 0.0 slice-done
  544.0 0.0 slice-done.1
  544.0 1.4 slice-done.2
  545.4 1.2 slice-done.3
  546.6 0.0 copy-start.6
  546.6 6.3 %copy.32 = bf16[2,4096,1024]{2,1,0:T(8,128)(2,1)} copy(bf16[2,4096,1024]{2,1,0:T(8,128)(2,1)S(1)} %bitcast.17) | data formatting | bytes 33554432
  552.9 0.0 copy-done.6
  552.9 0.0 copy-start.5
  552.9 1.3 copy.33
  554.2 1.0 copy-done.5
  555.2 0.0 copy-start.4
  555.2 1.3 copy.34
  556.6 1.0 copy-done.4
  557.6 0.0 copy-start.3
  557.6 1.3 copy.35
  558.9 1.0 copy-done.3
  559.9 0.0 copy-start.2
  559.9 1.3 copy.36
  561.3 1.0 copy-done.2
  562.3 0.0 copy-start.1
  562.3 1.3 copy.37
  563.6 1.0 copy-done.1
  564.6 1.3 copy.38
  (1 shorter events, 0.0 us)
Async XLA Ops:
  518.7 16.8 %copy-start = (bf16[2,4,4,64,4096]{4,3,2,1,0:T(8,128)(2,1)S(1)}, bf16[2,4,4,64,4096]{4,3,2,1,0:T(8,128)(2,1)}, u32[]{:S(2)}) copy-start(bf16[2,4,4,64,4096]{4,3,2,1,0:T(8,128)(2,1)} %get-tuple-element.19) | copy-start | bytes 50331652
  518.7 25.3 %slice-start = ((s8[16777216]{0:T(1024)(128)(4,1)}), s8[4194304]{0:T(1024)(128)(4,1)S(1)}, s32[]{:S(2)}) async-start(s8[16777216]{0:T(1024)(128)(4,1)} %bitcast.15), calls=%async_computation | async-start | bytes 8388608
  518.7 25.3 %slice-start.1 = ((s8[16777216]{0:T(1024)(128)(4,1)}), s8[4194304]{0:T(1024)(128)(4,1)S(1)}, s32[]{:S(2)}) async-start(s8[16777216]{0:T(1024)(128)(4,1)} %bitcast.15), calls=%async_computation.1 | async-start | bytes 8388608
  535.5 9.9 %slice-start.2 = ((s8[16777216]{0:T(1024)(128)(4,1)}), s8[4194304]{0:T(1024)(128)(4,1)S(1)}, s32[]{:S(2)}) async-start(s8[16777216]{0:T(1024)(128)(4,1)} %bitcast.15), calls=%async_computation.2 | async-start | bytes 8388608
  535.5 11.1 %slice-start.3 = ((s8[16777216]{0:T(1024)(128)(4,1)}), s8[4194304]{0:T(1024)(128)(4,1)S(1)}, s32[]{:S(2)}) async-start(s8[16777216]{0:T(1024)(128)(4,1)} %bitcast.15), calls=%async_computation.3 | async-start | bytes 8388608
  546.6 6.3 %copy-start.6 = (f32[2,64,4096]{2,1,0:T(8,128)S(1)}, f32[2,64,4096]{2,1,0:T(8,128)}, u32[]{:S(2)}) copy-start(f32[2,64,4096]{2,1,0:T(8,128)} %get-tuple-element.39) | copy-start | bytes 6291460
  552.9 2.3 copy-start.5
  555.2 2.3 copy-start.4
  557.6 2.3 copy-start.3
  559.9 2.3 copy-start.2
  562.3 2.3 copy-start.1
